TPU v7x, 32 devices: a whole 2x2x4 slice. The times are simulated.
32 devices in a mesh: blk: 32 (over z, y, x, core).
Axes of the slice: x: 2, y: 2, z: 4, core: 2. Of those that a mesh axis runs over, the one named last changes fastest.
Arguments:
- defect: float32 [384, 128], P('blk'), may hold values from -6 to 6
- mass: float32 [384, 128], P('blk'), may hold values from 1 to 2
- block_diag: float32 [384, 128, 128], P('blk'), may hold values from -0.1875 to 0.1875
- coupling: float32 [3072, 128, 128], P('blk'), may hold values from -0.09375 to 0.09375
- tile_rows: int32 [3072], P('blk'), may hold values from 0 to 383, as said below
- tile_cols: int32 [3072], P('blk'), may hold values from 0 to 383, as said below
Outputs:
- update: float32 [384, 128], P('blk')
Inputs may be any that keep to these rules, and one draw needn't show every extreme that they name: `tile_rows`: block rows d * 12 to d * 12 + 11 belong to device d of blk, and each device holds the tiles at positions d * 96 to d * 96 + 95. Of every tile a device holds, exactly one of its block row and block column belongs to that device; the other belongs to a different device. Exactly half of the 96 tiles of every device have their block row with that device, and the other half their block column. A program may send only the blocks and products of tiles that exist; slots of a padded buffer that no tile fills need not be sent. `tile_cols`: of one device's tiles, at most 2 have their block column with any one other device and at most 2 have their block row with any one other device; every device reaches 2 with some other device on each of the two sides.
All inputs are finite; a program needn't handle non-finite values.
Results may differ from a plain program's by a relative error of at most 0.0001.
Values sent between devices are 32-bit elements; how exact they have to be, the bound alone decides.
A program may use at most 64 MiB of HBM per device.

v0:
```python
import jax
import jax.numpy as jnp
from jax import lax
from jax.sharding import PartitionSpec as P

ITERS = 3


def solve_small(gram, target):
    factor = jnp.linalg.cholesky(gram)
    count = gram.shape[0]
    forward = []
    for index in range(count):
        value = target[index]
        for inner in range(index):
            value = value - factor[index, inner] * forward[inner]
        forward.append(value / factor[index, index])
    backward = [None] * count
    for index in reversed(range(count)):
        value = forward[index]
        for inner in range(index + 1, count):
            value = value - factor[inner, index] * backward[inner]
        backward[index] = value / factor[index, index]
    return backward


def tile_products(coupling, inputs):
    return jnp.einsum("tij,tj->ti", coupling, inputs, precision=lax.Precision.HIGHEST)


def row_sum(targets, values, rows_here):
    onehot = (jnp.arange(rows_here, dtype=jnp.int32)[:, None] == targets[None, :]).astype(
        jnp.float32
    )
    return jnp.dot(
        onehot, values, precision=lax.Precision.HIGHEST, preferred_element_type=jnp.float32
    )


def lane_slots(lanes, lane_count):
    onehot = (lanes[:, None] == jnp.arange(lane_count, dtype=jnp.int32)[None, :]).astype(jnp.int32)
    before = jnp.cumsum(onehot, axis=0) - onehot
    return jnp.sum(before * onehot, axis=1)


def on_device(defect, mass, block_diag, coupling, tile_rows, tile_cols):
    rows_here = defect.shape[0]
    width = defect.shape[1]
    tiles_here = tile_rows.shape[0]
    devices = lax.axis_size("blk")
    slots = (tiles_here // 2 + devices - 2) // (devices - 1)
    myself = lax.axis_index("blk")
    row_owner = tile_rows // rows_here
    col_owner = tile_cols // rows_here
    row_local = tile_rows % rows_here
    col_local = tile_cols % rows_here
    fetch_need = col_owner != myself
    push_need = row_owner != myself
    fetch_lane = jnp.where(fetch_need, col_owner, devices)
    push_lane = jnp.where(push_need, row_owner, devices)
    fetch_slot = lane_slots(fetch_lane, devices)
    push_slot = lane_slots(push_lane, devices)
    requests = (
        jnp.zeros((devices, slots), jnp.int32)
        .at[fetch_lane, fetch_slot]
        .set(col_local, mode="drop")
    )
    targets = (
        jnp.zeros((devices, slots), jnp.int32).at[push_lane, push_slot].set(row_local, mode="drop")
    )
    asked, landing = (
        lax.all_to_all(requests, "blk", split_axis=0, concat_axis=0, tiled=True),
        lax.all_to_all(targets, "blk", split_axis=0, concat_axis=0, tiled=True),
    )
    fetch_pick = jnp.minimum(fetch_lane, devices - 1)
    kept_rows = jnp.where(push_need, -1, row_local)
    landing_flat = landing.reshape(-1)
    negated = -defect
    beta = jnp.sqrt(lax.psum(jnp.sum(negated * negated), "blk"))
    basis = [negated / beta]
    upper = jnp.zeros((ITERS + 1, ITERS), jnp.float32)
    for column in range(ITERS):
        apply_vector = basis[column]
        fetched = lax.all_to_all(
            apply_vector[asked], "blk", split_axis=0, concat_axis=0, tiled=True
        )
        inputs = jnp.where(
            fetch_need[:, None], fetched[fetch_pick, fetch_slot], apply_vector[col_local]
        )
        products = tile_products(coupling, inputs)
        outgoing = (
            jnp.zeros((devices, slots, width), jnp.float32)
            .at[push_lane, push_slot]
            .set(products, mode="drop")
        )
        arrived = lax.all_to_all(outgoing, "blk", split_axis=0, concat_axis=0, tiled=True)
        local_rows = row_sum(kept_rows, products, rows_here)
        remote_rows = row_sum(landing_flat, arrived.reshape(-1, width), rows_here)
        own = jnp.einsum("rij,rj->ri", block_diag, apply_vector, precision=lax.Precision.HIGHEST)
        image = mass * apply_vector + own + local_rows + remote_rows
        local_dots = jnp.stack([jnp.sum(item * image) for item in basis])
        dots = lax.psum(local_dots, "blk")
        for index in range(column + 1):
            image = image - dots[index] * basis[index]
        norm = jnp.sqrt(lax.psum(jnp.sum(image * image), "blk"))
        upper = upper.at[: column + 1, column].set(dots)
        upper = upper.at[column + 1, column].set(norm)
        if column + 1 < ITERS:
            basis.append(image / norm)
    gram = jnp.dot(
        upper.T, upper, precision=lax.Precision.HIGHEST, preferred_element_type=jnp.float32
    )
    mixing = solve_small(gram, beta * upper[0, :])
    update = jnp.zeros_like(defect)
    for index in range(ITERS):
        update = update + mixing[index] * basis[index]
    return update


def solution(mesh):
    in_specs = (
        P("blk", None),
        P("blk", None),
        P("blk", None, None),
        P("blk", None, None),
        P("blk"),
        P("blk"),
    )
    out_specs = P("blk", None)
    return jax.shard_map(
        on_device, mesh=mesh, in_specs=in_specs, out_specs=out_specs, check_vma=False
    )
```

profile of v0, /device:TPU:0, one launch (start us, length us, event | category | flops | bytes accessed | tf_op | source)
XLA Modules:
  0.0 493.6 jit_solution(12215149020119974177)
XLA Ops:
  0.0 0.7 compare_select_fusion.3
  0.7 0.7 broadcast_compare_fusion
  1.4 0.7 compare_select_fusion.7
  2.5 5.0 %scatter_fusion = s32[32,2]{0,1:T(2,128)S(1)} fusion(s32[32,2]{0,1:T(2,128)S(1)} %broadcast.206.clone, s32[96]{0:T(128)S(1)} %get-tuple-element.102, s32[96]{0:T(128)S(1)} %get-tuple-element.91), kind=kCustom, calls=%fused_computation.9 | custom fusion | bytes 1920 | tf_op jit(solution)/shard_map/scatter | solution.py:66
  7.5 0.7 copy.13
  8.2 1.3 multiply_reduce_fusion.9
  9.5 7.3 %all-to-all-start = ((s32[32,1,2]{2,1,0:T(1,128)}), s32[32,1,2]{2,1,0:T(1,128)S(1)}, u32[]{:S(2)}, u32[]{:S(2)}) async-start(s32[32,1,2]{2,1,0:T(1,128)} %copy.13), calls=%async_computation | async-start | bytes 32768 | tf_op jit(solution)/shard_map/all_to_all | solution.py:72
  16.8 40.7 %psum.49 = f32[]{:T(128)} all-reduce(f32[]{:T(128)} %multiply_reduce_fusion.9), channel_id=1, replica_groups=mesh['blk'=32] {'blk'}, use_global_device_ids=true, to_apply=%region_1.2 | all-reduce | flops 1 | bytes 8 | tf_op jit(solution)/shard_map/psum | solution.py:79
  58.2 0.7 negate_divide_fusion
  58.9 0.7 fusion.54
  59.6 0.7 compare_select_fusion.8
  61.3 1.4 and_reduce_fusion
  62.7 1.3 fusion.6
  64.0 5.0 %scatter_fusion.1 = s32[32,2]{0,1:T(2,128)S(1)} fusion(s32[32,2]{0,1:T(2,128)S(1)} %broadcast.206.clone.1, s32[96]{0:T(128)S(1)} %fusion.24, s32[96]{0:T(128)S(1)} %get-tuple-element.87), kind=kCustom, calls=%fused_computation.10 | custom fusion | bytes 1920 | tf_op jit(solution)/shard_map/scatter | solution.py:69
  69.0 0.7 copy.16
  70.3 4.7 all-to-all-start.2
  75.3 1.2 gather_fusion
  76.5 5.7 %all-to-all-done.2 = s32[32,1,2]{2,1,0:T(1,128)S(1)} async-done(((s32[32,1,2]{2,1,0:T(1,128)}), s32[32,1,2]{2,1,0:T(1,128)S(1)}, u32[]{:S(2)}, u32[]{:S(2)}) %all-to-all-start.2) | async-done | bytes 288 | tf_op jit(solution)/shard_map/all_to_all | solution.py:73
  82.2 2.6 all-to-all-start.1
  85.9 0.7 reduce.33
  86.7 5.3 %all-to-all-done.1 = f32[32,2,128]{2,1,0:T(2,128)S(1)} async-done(((f32[32,2,128]{2,1,0:T(2,128)}), f32[32,2,128]{2,1,0:T(2,128)S(1)}, u32[]{:S(2)}, u32[]{:S(2)}) %all-to-all-start.1) | async-done | bytes 32800 | tf_op jit(solution)/shard_map/all_to_all | solution.py:84
  92.0 1.2 gather_fusion.1
  93.3 11.8 %fusion.32 = f32[96,1,128]{2,1,0:T(1,128)S(1)} fusion(f32[96,128,1]{1,2,0:T(1,128)S(1)} %bitcast.142, f32[96,128,128]{2,1,0:T(8,128)} %param.21), kind=kOutput, calls=%fused_computation.117 | convolution fusion | flops 18874368 | bytes 6389760 | tf_op jit(solution)/shard_map/tij,tj->ti/dot_general | solution.py:28
  105.8 11.3 %scatter_fusion.2 = f32[32,2,128]{2,1,0:T(2,128)} fusion(f32[32,2,128]{2,1,0:T(2,128)} %broadcast.211.clone, s32[96]{0:T(128)S(1)} %fusion.24, f32[96,128]{1,0:T(8,128)S(1)} %bitcast.137), kind=kCustom, calls=%fused_computation.11 | custom fusion | bytes 148224 | tf_op jit(solution)/shard_map/scatter | solution.py:94
  117.1 2.6 all-to-all-start.3
  119.8 7.1 %all-to-all-done.3 = f32[32,2,128]{2,1,0:T(2,128)S(1)} async-done(((f32[32,2,128]{2,1,0:T(2,128)}), f32[32,2,128]{2,1,0:T(2,128)S(1)}, u32[]{:S(2)}, u32[]{:S(2)}) %all-to-all-start.3) | async-done | bytes 32800 | tf_op jit(solution)/shard_map/all_to_all | solution.py:96
  126.9 0.7 multiply_reduce_fusion.8
  127.6 38.4 %psum.50 = f32[1]{0:T(128)} all-reduce(f32[1]{0:T(128)} %bitcast.19), channel_id=1, replica_groups=mesh['blk'=32] {'blk'}, use_global_device_ids=true, to_apply=%region_10.11 | all-reduce | flops 1 | bytes 8 | tf_op jit(solution)/shard_map/psum | solution.py:102
  166.1 1.3 multiply_reduce_fusion.7
  168.0 40.4 %psum.51 = f32[]{:T(128)} all-reduce(f32[]{:T(128)} %multiply_reduce_fusion.7), channel_id=1, replica_groups=mesh['blk'=32] {'blk'}, use_global_device_ids=true, to_apply=%region_12.13 | all-reduce | flops 1 | bytes 8 | tf_op jit(solution)/shard_map/psum | solution.py:105
  209.9 1.2 gather_fusion.3
  211.1 5.0 %all-to-all-start.4 = ((f32[32,2,128]{2,1,0:T(2,128)}), f32[32,2,128]{2,1,0:T(2,128)S(1)}, u32[]{:S(2)}, u32[]{:S(2)}) async-start(f32[32,2,128]{2,1,0:T(2,128)} %bitcast.25), calls=%async_computation.4 | async-start | bytes 65536 | tf_op jit(solution)/shard_map/all_to_all | solution.py:84
  216.1 1.3 fusion.4
  218.7 4.5 all-to-all-done.4
  223.2 1.2 gather_fusion.4
  224.5 11.8 %fusion.33 = f32[96,1,128]{2,1,0:T(1,128)S(1)} fusion(f32[96,128,1]{1,2,0:T(1,128)S(1)} %bitcast.143, f32[96,128,128]{2,1,0:T(8,128)} %param.21), kind=kOutput, calls=%fused_computation.118 | convolution fusion | flops 18874368 | bytes 6389760 | tf_op jit(solution)/shard_map/tij,tj->ti/dot_general | solution.py:28
  237.0 11.3 %scatter_fusion.3 = f32[32,2,128]{2,1,0:T(2,128)} fusion(f32[32,2,128]{2,1,0:T(2,128)} %broadcast.211.clone.1, s32[96]{0:T(128)S(1)} %fusion.24, f32[96,128]{1,0:T(8,128)S(1)} %bitcast.139), kind=kCustom, calls=%fused_computation.12 | custom fusion | bytes 148224 | tf_op jit(solution)/shard_map/scatter | solution.py:94
  248.2 2.6 all-to-all-start.5
  250.9 7.1 %all-to-all-done.5 = f32[32,2,128]{2,1,0:T(2,128)S(1)} async-done(((f32[32,2,128]{2,1,0:T(2,128)}), f32[32,2,128]{2,1,0:T(2,128)S(1)}, u32[]{:S(2)}, u32[]{:S(2)}) %all-to-all-start.5) | async-done | bytes 32800 | tf_op jit(solution)/shard_map/all_to_all | solution.py:96
  258.1 0.8 multiply_reduce_fusion.6
  258.9 1.4 pad_maximum_fusion
  260.4 38.3 %psum.52 = f32[2]{0:T(128)S(1)} all-reduce(f32[2]{0:T(128)S(1)} %pad_maximum_fusion), channel_id=1, replica_groups=mesh['blk'=32] {'blk'}, use_global_device_ids=true, to_apply=%region_17.18 | all-reduce | flops 2 | bytes 16 | tf_op jit(solution)/shard_map/psum | solution.py:102
  298.7 0.7 fusion.31
  299.3 2.0 multiply_reduce_fusion.4
  301.3 40.2 %psum.53 = f32[]{:T(128)} all-reduce(f32[]{:T(128)} %get-tuple-element.82), channel_id=1, replica_groups=mesh['blk'=32] {'blk'}, use_global_device_ids=true, to_apply=%region_19.20 | all-reduce | flops 1 | bytes 8 | tf_op jit(solution)/shard_map/psum | solution.py:105
  342.3 1.2 gather_fusion.6
  343.5 5.0 %all-to-all-start.6 = ((f32[32,2,128]{2,1,0:T(2,128)}), f32[32,2,128]{2,1,0:T(2,128)S(1)}, u32[]{:S(2)}, u32[]{:S(2)}) async-start(f32[32,2,128]{2,1,0:T(2,128)} %bitcast.41), calls=%async_computation.6 | async-start | bytes 65536 | tf_op jit(solution)/shard_map/all_to_all | solution.py:84
  348.5 1.3 fusion.2
  349.8 1.8 broadcast_select_fusion.4
  352.3 3.3 all-to-all-done.6
  355.5 1.2 gather_fusion.7
  356.8 11.8 %fusion.34 = f32[96,1,128]{2,1,0:T(1,128)S(1)} fusion(f32[96,128,1]{1,2,0:T(1,128)S(1)} %bitcast.141, f32[96,128,128]{2,1,0:T(8,128)} %param.21), kind=kOutput, calls=%fused_computation.119 | convolution fusion | flops 18874368 | bytes 6389760 | tf_op jit(solution)/shard_map/tij,tj->ti/dot_general | solution.py:28
  369.3 11.3 %scatter_fusion.4 = f32[32,2,128]{2,1,0:T(2,128)} fusion(f32[32,2,128]{2,1,0:T(2,128)} %broadcast.211, s32[96]{0:T(128)S(1)} %fusion.24, f32[96,128]{1,0:T(8,128)S(1)} %bitcast.135), kind=kCustom, calls=%fused_computation.13 | custom fusion | bytes 148224 | tf_op jit(solution)/shard_map/scatter | solution.py:94
  380.6 2.6 all-to-all-start.7
  383.3 7.1 %all-to-all-done.7 = f32[32,2,128]{2,1,0:T(2,128)S(1)} async-done(((f32[32,2,128]{2,1,0:T(2,128)}), f32[32,2,128]{2,1,0:T(2,128)S(1)}, u32[]{:S(2)}, u32[]{:S(2)}) %all-to-all-start.7) | async-done | bytes 32800 | tf_op jit(solution)/shard_map/all_to_all | solution.py:96
  390.4 0.8 multiply_reduce_fusion.3
  391.2 2.0 pad_maximum_fusion.1
  393.2 1.3 scatter.71
  394.5 38.3 %psum.54 = f32[3]{0:T(128)S(1)} all-reduce(f32[3]{0:T(128)S(1)} %pad_maximum_fusion.1), channel_id=1, replica_groups=mesh['blk'=32] {'blk'}, use_global_device_ids=true, to_apply=%region_25.26 | all-reduce | flops 3 | bytes 24 | tf_op jit(solution)/shard_map/psum | solution.py:102
  432.8 0.7 fusion.28
  433.5 2.5 multiply_reduce_fusion
  436.1 40.2 %psum.55 = f32[]{:T(128)} all-reduce(f32[]{:T(128)} %multiply_reduce_fusion), channel_id=1, replica_groups=mesh['blk'=32] {'blk'}, use_global_device_ids=true, to_apply=%region_27.28 | all-reduce | flops 1 | bytes 8 | tf_op jit(solution)/shard_map/psum | solution.py:105
  477.0 1.9 broadcast_select_fusion.3
  479.0 1.4 scatter.74
  (60 shorter events, 13.2 us)
Async XLA Ops:
  0.0 62.7 %copy-start = (f32[12,128,128]{2,1,0:T(8,128)S(1)}, f32[12,128,128]{2,1,0:T(8,128)}, u32[]{:S(2)}) copy-start(f32[12,128,128]{2,1,0:T(8,128)} %param.20) | copy-start | bytes 2359300
  0.0 119.7 %copy-start.2 = (f32[12,128]{1,0:T(8,128)S(1)}, f32[12,128]{1,0:T(8,128)}, u32[]{:S(2)}) copy-start(f32[12,128]{1,0:T(8,128)} %param.19) | copy-start | bytes 18436
  2.3 163.8 %copy-start.1 = (f32[12,128]{1,0:T(8,128)S(1)}, f32[12,128]{1,0:T(8,128)}, u32[]{:S(2)}) copy-start(f32[12,128]{1,0:T(8,128)} %param.18) | copy-start | bytes 18436
  9.5 60.8 %all-to-all-start = ((s32[32,1,2]{2,1,0:T(1,128)}), s32[32,1,2]{2,1,0:T(1,128)S(1)}, u32[]{:S(2)}, u32[]{:S(2)}) async-start(s32[32,1,2]{2,1,0:T(1,128)} %copy.13), calls=%async_computation | async-start | bytes 32768 | tf_op jit(solution)/shard_map/all_to_all | solution.py:72
  70.3 11.9 %all-to-all-start.2 = ((s32[32,1,2]{2,1,0:T(1,128)}), s32[32,1,2]{2,1,0:T(1,128)S(1)}, u32[]{:S(2)}, u32[]{:S(2)}) async-start(s32[32,1,2]{2,1,0:T(1,128)} %copy.16), calls=%async_computation.2 | async-start | bytes 32768 | tf_op jit(solution)/shard_map/all_to_all | solution.py:73
  82.2 9.8 %all-to-all-start.1 = ((f32[32,2,128]{2,1,0:T(2,128)}), f32[32,2,128]{2,1,0:T(2,128)S(1)}, u32[]{:S(2)}, u32[]{:S(2)}) async-start(f32[32,2,128]{2,1,0:T(2,128)} %bitcast.7), calls=%async_computation.1 | async-start | bytes 65536 | tf_op jit(solution)/shard_map/all_to_all | solution.py:84
  117.1 9.8 %all-to-all-start.3 = ((f32[32,2,128]{2,1,0:T(2,128)}), f32[32,2,128]{2,1,0:T(2,128)S(1)}, u32[]{:S(2)}, u32[]{:S(2)}) async-start(f32[32,2,128]{2,1,0:T(2,128)} %scatter_fusion.2), calls=%async_computation.3 | async-start | bytes 65536 | tf_op jit(solution)/shard_map/all_to_all | solution.py:96
  211.1 12.1 %all-to-all-start.4 = ((f32[32,2,128]{2,1,0:T(2,128)}), f32[32,2,128]{2,1,0:T(2,128)S(1)}, u32[]{:S(2)}, u32[]{:S(2)}) async-start(f32[32,2,128]{2,1,0:T(2,128)} %bitcast.25), calls=%async_computation.4 | async-start | bytes 65536 | tf_op jit(solution)/shard_map/all_to_all | solution.py:84
  248.2 9.8 %all-to-all-start.5 = ((f32[32,2,128]{2,1,0:T(2,128)}), f32[32,2,128]{2,1,0:T(2,128)S(1)}, u32[]{:S(2)}, u32[]{:S(2)}) async-start(f32[32,2,128]{2,1,0:T(2,128)} %scatter_fusion.3), calls=%async_computation.5 | async-start | bytes 65536 | tf_op jit(solution)/shard_map/all_to_all | solution.py:96
  343.5 12.0 %all-to-all-start.6 = ((f32[32,2,128]{2,1,0:T(2,128)}), f32[32,2,128]{2,1,0:T(2,128)S(1)}, u32[]{:S(2)}, u32[]{:S(2)}) async-start(f32[32,2,128]{2,1,0:T(2,128)} %bitcast.41), calls=%async_computation.6 | async-start | bytes 65536 | tf_op jit(solution)/shard_map/all_to_all | solution.py:84
  380.6 9.8 %all-to-all-start.7 = ((f32[32,2,128]{2,1,0:T(2,128)}), f32[32,2,128]{2,1,0:T(2,128)S(1)}, u32[]{:S(2)}, u32[]{:S(2)}) async-start(f32[32,2,128]{2,1,0:T(2,128)} %scatter_fusion.4), calls=%async_computation.7 | async-start | bytes 65536 | tf_op jit(solution)/shard_map/all_to_all | solution.py:96
where the time goes:
time: 496 us; the launch traced here: 494 us
  blocking collectives  277 us (56%)
  local copies, waits for them, and re-layouts  64.5 us (13%)
  matrix products  42.4 us (9%)
  waiting for transfers between devices  40.1 us (8%)
  starting transfers between devices  32.3 us (7%)
  other arithmetic  25.1 us (5%)
  between operations  12.6 us (3%)
    psum x3, blocking collectives, on_device(): norm = jnp.sqrt(lax.psum(jnp.sum(image * image), 'blk'))  121 us
    psum x3, blocking collectives, on_device(): dots = lax.psum(local_dots, 'blk')  115 us
    psum x1, blocking collectives, on_device(): beta = jnp.sqrt(lax.psum(jnp.sum(negated * negated), 'blk'))  40.7 us
    dot_general x3, matrix products, tile_products(): jnp.einsum('tij,tj->ti', coupling, inputs, precision=lax.Precision.HIGHEST)  35.5 us
    scatter x3, local copies, waits for them, and re-layouts, on_device(): outgoing = jnp.zeros((devices, slots, width), jnp.float32).at[push_lane,...  33.8 us
    all_to_all x3, waiting for transfers between devices, on_device(): lax.all_to_all(outgoing, 'blk', split_axis=0, concat_axis=0, tiled=True)  21.4 us
    all_to_all x3, waiting for transfers between devices, on_device(): lax.all_to_all(apply_vector[asked], 'blk', split_axis=0, concat_axis=0, t...  13.1 us
    all_to_all x3, starting transfers between devices, on_device(): lax.all_to_all(apply_vector[asked], 'blk', split_axis=0, concat_axis=0, t...  12.6 us
  transfers between devices with their start and end apart: 8, of which 7 were waited for; matrix products, arithmetic and copies ran while one was open for 5% of the time, Pallas kernels for 0%

commit v1 on v0

v1 whole, which is shorter than its diff:
```python
import functools

import jax
import jax.numpy as jnp
from jax import lax
from jax.experimental import pallas as pl
from jax.experimental.pallas import tpu as pltpu
from jax.sharding import PartitionSpec as P

ITERS = 3
F32 = jnp.float32
MESH = pl.DeviceIdType.MESH
STEP = 12


def iota(shape, axis):
    return lax.broadcasted_iota(jnp.int32, shape, axis)


def iota_f(shape, axis):
    return iota(shape, axis).astype(F32)


def dot(a, b):
    return lax.dot_general(
        a,
        b,
        (((1,), (0,)), ((), ())),
        precision=lax.Precision.HIGHEST,
        preferred_element_type=F32,
    )


def total(value):
    return jnp.sum(jnp.sum(value, axis=0, keepdims=True), axis=1, keepdims=True)


def as_row(items):
    lane = iota((1, 128), 1)
    row = jnp.zeros((1, 128), F32)
    for index, item in enumerate(items):
        row = jnp.where(lane == index, item, row)
    return row


def pick(row, index):
    lane = iota((1, 128), 1)
    return jnp.sum(jnp.where(lane == index, row, 0.0), axis=1, keepdims=True)


def kernel(
    n,
    slots,
    defect_ref,
    mass_ref,
    diag_hbm,
    coup_hbm,
    rows_ref,
    cols_ref,
    out_ref,
    coup,
    diag,
    order_v,
    order_s,
    mass16,
    wbuf,
    xbuf,
    ask_hot,
    land_hot,
    send0,
    recv0,
    send_a,
    recv_a,
    send_b,
    recv_b,
    send_f,
    recv_f,
    load_sems,
    order_sem,
    sent,
    got,
):
    me = lax.axis_index("blk")
    rb, width = defect_ref.shape
    tiles = rows_ref.shape[1]
    half = tiles // 2
    pad = wbuf.shape[0]
    head = send0.shape[0]
    parts = 4
    chunk = tiles // parts

    loads = [pltpu.make_async_copy(diag_hbm, diag, load_sems.at[parts])]
    for part in range(parts):
        span = pl.ds(part * chunk, chunk)
        loads.append(
            pltpu.make_async_copy(coup_hbm.at[span], coup.at[span], load_sems.at[part])
        )
    for item in loads:
        item.start()

    barrier = pltpu.get_barrier_semaphore()

    def greet(k, carry):
        pl.semaphore_signal(
            barrier, inc=1, device_id=(lax.rem(me + k, n),), device_id_type=MESH
        )
        return carry

    lax.fori_loop(1, n, greet, 0)

    rows = rows_ref[...]
    cols = cols_ref[...]
    low = me * rb
    pushes = (rows < low) | (rows >= low + rb)
    push_l = jnp.where(pushes, 1.0, 0.0)
    rem_l = jnp.where(pushes, rows, cols).astype(F32)
    loc_l = (jnp.where(pushes, cols, rows) - low).astype(F32)
    own_l = jnp.floor((rem_l + 0.5) * (1.0 / rb))
    far_l = rem_l - own_l * rb
    me_f = me.astype(F32)
    rel_l = own_l - me_f - 1.0
    rel_l = jnp.where(rel_l < 0.0, rel_l + n, rel_l)
    key_l = own_l + push_l * n
    square = (tiles, tiles)
    eye = iota(square, 0) == iota(square, 1)

    def to_s(value):
        return jnp.sum(jnp.where(eye, value, 0.0), axis=1, keepdims=True)

    earlier = iota(square, 0) < iota(square, 1)
    key_s = to_s(key_l)
    push_s = to_s(push_l)
    slot_l = jnp.sum(
        jnp.where((key_s == key_l) & earlier, 1.0, 0.0), axis=0, keepdims=True
    )
    pos_l = jnp.sum(
        jnp.where((push_s < push_l) | ((push_s == push_l) & earlier), 1.0, 0.0),
        axis=0,
        keepdims=True,
    )
    pos_s = to_s(pos_l)
    slot_s = to_s(slot_l)
    own_s = to_s(own_l)
    far_s = to_s(far_l)
    loc_s = to_s(loc_l)
    u_l = rel_l * 8.0 + slot_l
    u_s = to_s(u_l)
    wide = (tiles, 128)
    lane_w = iota_f(wide, 1)
    push_int = jnp.where(pushes, 1, 0)
    push_down = jnp.sum(jnp.where(eye, push_int, 0), axis=1, keepdims=True)
    place = jnp.sum(
        jnp.where(
            (push_down < push_int) | ((push_down == push_int) & earlier), 1, 0
        ),
        axis=0,
        keepdims=True,
    )
    place_down = jnp.sum(jnp.where(eye, place, 0), axis=1, keepdims=True)
    order_v[...] = jnp.sum(
        jnp.where(place_down == iota(wide, 1), iota(wide, 0), 0), axis=0, keepdims=True
    )
    order_copy = pltpu.make_async_copy(order_v, order_s, order_sem)
    order_copy.start()
    lane_1 = iota_f((1, 128), 1)
    push_u = jnp.sum(jnp.where(pos_s == lane_w + half, u_s, 0.0), axis=0, keepdims=True)
    push_u = jnp.where(lane_1 < half, push_u, -1.0)
    fetch_row = jnp.sum(jnp.where(pos_s == lane_w, loc_s, 0.0), axis=0, keepdims=True)
    fetch_row = jnp.where(lane_1 < half, fetch_row, -1.0)
    sorted_shape = (half, tiles)
    fetch_here = pos_l == iota_f(sorted_shape, 0)
    push_here = pos_l == iota_f(sorted_shape, 0) + half
    fetch_u = jnp.sum(jnp.where(fetch_here, u_l, 0.0), axis=1, keepdims=True)
    fetch_v = jnp.sum(
        jnp.where(fetch_here, rel_l * head + far_l, 0.0), axis=1, keepdims=True
    )
    push_col = jnp.sum(jnp.where(push_here, loc_l, 0.0), axis=1, keepdims=True)
    lane_key = own_s * slots + slot_s
    asks = jnp.sum(
        jnp.where((lane_key == lane_w) & (push_s < 0.5), far_s + 1.0, 0.0),
        axis=0,
        keepdims=True,
    ) - 1.0
    goals = jnp.sum(
        jnp.where((lane_key == lane_w) & (push_s > 0.5), far_s + 1.0, 0.0),
        axis=0,
        keepdims=True,
    ) - 1.0
    slots8 = n * 8

    def hot(mask):
        return jnp.where(mask, 1.0, 0.0)

    wbuf[...] = jnp.zeros(wbuf.shape, F32)
    wbuf[0:rb, :] = -defect_ref[...]
    mass16[...] = jnp.zeros(mass16.shape, F32)
    mass16[0:rb, :] = mass_ref[...]
    vector = wbuf[...]
    send0[...] = jnp.zeros(send0.shape, F32)
    send0[0:rb, :] = -defect_ref[...]
    own_part = as_row([total(vector * vector)])
    send0[rb : rb + 1, :] = own_part
    send0[rb + 1 : rb + 2, :] = asks
    send0[rb + 2 : rb + 3, :] = goals
    recv0[n - 1] = jnp.zeros(recv0.shape[1:], F32)
    for turn in range(ITERS):
        recv_b[turn, n - 1] = jnp.zeros((8, 128), F32)
    for turn in range(ITERS - 1):
        recv_a[turn, n - 1] = jnp.zeros((8, 128), F32)
    recv_f[n - 1] = jnp.zeros((8, 128), F32)

    pl.semaphore_wait(barrier, n - 1)

    def broadcast(source, target, index, spread):
        def one(k, carry):
            pltpu.make_async_remote_copy(
                src_ref=source.at[k - 1] if spread else source,
                dst_ref=target.at[n - 1 - k],
                send_sem=sent.at[index],
                recv_sem=got.at[index],
                device_id=(lax.rem(me + k, n),),
                device_id_type=MESH,
            ).start()
            return carry

        lax.fori_loop(1, n, one, 0)

    def await_all(target, sem):
        view = target.at[pl.ds(0, n - 1)]
        pltpu.make_async_copy(view, view, sem).wait()

    broadcast(send0, recv0, 0, False)

    spread_hot = hot(iota_f((slots8, 128), 0) == push_u)
    fetch_hot = hot(iota_f((half, slots8), 1) == fetch_u)
    first_hot = hot(iota_f((half, n * head), 1) == fetch_v)
    input_hot = hot(iota_f((half, pad), 1) == push_col)
    kept_hot = hot(iota_f((pad, 128), 0) == fetch_row)

    lane_k = iota((width, 128), 1)

    def matvec(acc, tile, index):
        row = xbuf[pl.ds(index, 1), :]
        value = jnp.sum(tile * row, axis=1, keepdims=True)
        return jnp.where(lane_k == index, value, acc)

    def coupled(base, acc):
        def body(step, acc):
            for inner in range(STEP):
                index = step * STEP + inner
                tile = jnp.clip(order_s[0, base + index], 0, 2 * half - 1)
                acc = matvec(acc, coup[tile], index)
            return acc

        return lax.fori_loop(0, half // STEP, body, acc)

    empty = jnp.zeros((width, 128), F32)

    def begin(turn, vector):
        xbuf[0:half, :] = dot(input_hot, vector)
        xbuf[half : half + pad, :] = vector
        acc = empty
        for index in range(rb):
            acc = matvec(acc, diag[index], half + index)
        acc = coupled(half, acc)
        found = acc.T
        send_b[turn] = dot(spread_hot, found).reshape(n, 8, 128)
        broadcast(send_b.at[turn], recv_b.at[turn], 1 + 2 * turn, True)
        return mass16[...] * vector + found[half : half + pad, :]

    def finish(turn, image, inputs):
        xbuf[0:half, :] = inputs
        found = coupled(0, empty).T
        image = image + dot(kept_hot, found)
        await_all(recv_b.at[turn], got.at[1 + 2 * turn])
        arrived = recv_b[turn].reshape(slots8, 128)
        return image + dot(land_hot[...], arrived)

    for item in loads:
        item.wait()
    order_copy.wait()

    image = begin(0, vector)
    await_all(recv0, got.at[0])
    lane_3 = iota((n, 8, 128), 2)
    sub_3 = iota((n, 8, 128), 1)
    peer_3 = iota((n, 8, 128), 0)
    mine = (lane_3 == me * slots + sub_3) & (sub_3 < slots) & (peer_3 < n - 1)

    def addressed(offset):
        line = recv0[:, rb + offset : rb + offset + 1, :]
        line = jnp.broadcast_to(line, (n, 8, 128))
        found = jnp.sum(jnp.where(mine, line + 1.0, 0.0), axis=2, keepdims=True) - 1.0
        return hot(found == lane_3.astype(F32)).reshape(slots8, 128)

    land_hot[...] = addressed(2).T[0:pad, :]
    ask_hot[...] = addressed(1)
    squares = jnp.sum(recv0[:, rb, :], axis=0, keepdims=True) + own_part
    beta = jnp.sqrt(pick(squares, 0))
    inputs = dot(first_hot, recv0[...].reshape(n * head, 128))
    image = finish(0, image, inputs)
    basis = [vector / beta]
    images = [image / beta]
    heads = []
    gram = {}

    for turn in range(1, ITERS):
        vector = images[-1]
        own_part = as_row(
            [total(vector * item) for item in basis]
            + [total(vector * item) for item in images]
        )
        wide_vector = jnp.concatenate([vector, jnp.zeros((128 - pad, 128), F32)], axis=0)
        blocks = dot(ask_hot[...], wide_vector).reshape(n, 8, 128)
        sub = iota((n, 8, 128), 1)
        blocks = jnp.where(sub == slots, own_part.reshape(1, 1, 128), blocks)
        send_a[turn - 1] = blocks
        broadcast(send_a.at[turn - 1], recv_a.at[turn - 1], 2 * turn, True)
        image = begin(turn, vector)
        await_all(recv_a.at[turn - 1], got.at[2 * turn])
        sums = jnp.sum(recv_a[turn - 1][:, slots, :], axis=0, keepdims=True) + own_part
        inputs = dot(fetch_hot, recv_a[turn - 1].reshape(slots8, 128))
        image = finish(turn, image, inputs)
        dots = [pick(sums, index) for index in range(turn)]
        for index in range(turn):
            gram[index, turn - 1] = pick(sums, turn + index)
        heads.append(dots[0])
        square = gram[turn - 1, turn - 1]
        left = square
        for value in dots:
            left = left - value * value
        scale = lax.rsqrt(jnp.maximum(left, square * 1e-6))
        for index in range(turn):
            vector = vector - dots[index] * basis[index]
            image = image - dots[index] * images[index]
        basis.append(vector * scale)
        images.append(image * scale)

    vector = images[-1]
    own_part = as_row(
        [total(vector * basis[0])] + [total(vector * item) for item in images]
    )
    send_f[...] = jnp.broadcast_to(own_part, (8, 128))
    broadcast(send_f, recv_f, 2 * ITERS, False)
    await_all(recv_f, got.at[2 * ITERS])
    sums = jnp.sum(recv_f[:, 0, :], axis=0, keepdims=True) + own_part
    heads.append(pick(sums, 0))
    for index in range(ITERS):
        gram[index, ITERS - 1] = pick(sums, 1 + index)

    factor = {}
    for i in range(ITERS):
        for j in range(i + 1):
            value = gram[j, i]
            for k in range(j):
                value = value - factor[i, k] * factor[j, k]
            factor[i, j] = jnp.sqrt(value) if i == j else value / factor[j, j]
    forward = []
    for i in range(ITERS):
        value = beta * heads[i]
        for k in range(i):
            value = value - factor[i, k] * forward[k]
        forward.append(value / factor[i, i])
    mixing = [None] * ITERS
    for i in reversed(range(ITERS)):
        value = forward[i]
        for k in range(i + 1, ITERS):
            value = value - factor[k, i] * mixing[k]
        mixing[i] = value / factor[i, i]
    update = mixing[0] * basis[0]
    for i in range(1, ITERS):
        update = update + mixing[i] * basis[i]
    out_ref[...] = update[0:rb, :]

    await_all(recv0, sent.at[0])
    for turn in range(ITERS):
        await_all(send_b.at[turn], sent.at[1 + 2 * turn])
    for turn in range(1, ITERS):
        await_all(send_a.at[turn - 1], sent.at[2 * turn])
    await_all(recv_f, sent.at[2 * ITERS])


def on_device(defect, mass, block_diag, coupling, tile_rows, tile_cols):
    rb, width = defect.shape
    tiles = tile_rows.shape[0]
    n = lax.axis_size("blk")
    slots = (tiles // 2 + n - 2) // (n - 1)
    pad = -(-rb // 8) * 8
    head = -(-(rb + 3) // 8) * 8
    vmem = pl.BlockSpec(memory_space=pltpu.VMEM)
    hbm = pl.BlockSpec(memory_space=pl.ANY)
    return pl.pallas_call(
        functools.partial(kernel, n, slots),
        out_shape=jax.ShapeDtypeStruct((rb, width), F32),
        in_specs=[vmem, vmem, hbm, hbm, vmem, vmem],
        out_specs=vmem,
        scratch_shapes=[
            pltpu.VMEM((tiles, width, width), F32),
            pltpu.VMEM((rb, width, width), F32),
            pltpu.VMEM((1, 128), jnp.int32),
            pltpu.SMEM((1, 128), jnp.int32),
            pltpu.VMEM((pad, width), F32),
            pltpu.VMEM((pad, width), F32),
            pltpu.VMEM((tiles, width), F32),
            pltpu.VMEM((n * 8, 128), F32),
            pltpu.VMEM((pad, n * 8), F32),
            pltpu.VMEM((head, width), F32),
            pltpu.VMEM((n, head, width), F32),
            pltpu.VMEM((ITERS - 1, n, 8, width), F32),
            pltpu.VMEM((ITERS - 1, n, 8, width), F32),
            pltpu.VMEM((ITERS, n, 8, width), F32),
            pltpu.VMEM((ITERS, n, 8, width), F32),
            pltpu.VMEM((8, width), F32),
            pltpu.VMEM((n, 8, width), F32),
            pltpu.SemaphoreType.DMA((5,)),
            pltpu.SemaphoreType.DMA,
            pltpu.SemaphoreType.DMA((2 * ITERS + 1,)),
            pltpu.SemaphoreType.DMA((2 * ITERS + 1,)),
        ],
        compiler_params=pltpu.CompilerParams(collective_id=0, has_side_effects=True),
    )(
        defect,
        mass,
        block_diag,
        coupling,
        tile_rows.reshape(1, tiles),
        tile_cols.reshape(1, tiles),
    )


def solution(mesh):
    in_specs = (
        P("blk", None),
        P("blk", None),
        P("blk", None, None),
        P("blk", None, None),
        P("blk"),
        P("blk"),
    )
    return jax.shard_map(
        on_device, mesh=mesh, in_specs=in_specs, out_specs=P("blk", None), check_vma=False
    )
```

time: 496 us -> 44.6 us (0.09)
  blocking collectives: 277 us -> 0 us
  local copies, waits for them, and re-layouts: 64.5 us -> 1.3 us
  Pallas kernels: 0 us -> 43.1 us
  matrix products: 42.4 us -> 0 us
  waiting for transfers between devices: 40.1 us -> 0 us
  starting transfers between devices: 32.3 us -> 0 us
  other arithmetic: 25.1 us -> 0 us
  between operations: 12.6 us -> 0.01 us
    psum x7 -> x0, blocking collectives: 277 us -> none  [the longest x3 121 us: on_device(): norm = jnp.sqrt(lax.psum(jnp.sum(image * image), 'blk'))]
    scatter x11 -> x0, local copies, waits for them, and re-layouts: 47.4 us -> none  [the longest x3 33.8 us: on_device(): outgoing = jnp.zeros((devices, slots, width), jnp.float32).at[push_lane,...]
    pallas_call x0 -> x1, Pallas kernels: none -> 43.1 us  [on_device(): pl.pallas_call(functools.partial(kernel, n, slots), out_shape=jax.ShapeDt...]
    dot_general x13 -> x0, matrix products: 42.4 us -> none  [the longest x3 35.5 us: tile_products(): jnp.einsum('tij,tj->ti', coupling, inputs, precision=lax.Precision.HIGHEST)]
    all_to_all x8 -> x0, waiting for transfers between devices: 40.1 us -> none  [the longest x3 21.4 us: on_device(): lax.all_to_all(outgoing, 'blk', split_axis=0, concat_axis=0, tiled=True)]
    all_to_all x8 -> x0, starting transfers between devices: 32.3 us -> none  [the longest x3 12.6 us: on_device(): lax.all_to_all(apply_vector[asked], 'blk', split_axis=0, concat_axis=0, t...]
    another operation x12 -> x0, other arithmetic: 10.4 us -> none
    gather x9 -> x0, local copies, waits for them, and re-layouts: 9.11 us -> none  [the longest x3 3.7 us: on_device(): fetched[fetch_pick, fetch_slot]]
  transfers between devices with their start and end apart: 8 -> 0, of which waited for: 7 -> 0; matrix products, arithmetic and copies ran while one was open for 5% -> 0% of each run, Pallas kernels for 0% -> 0%
where the time goes in v1:
time: 44.6 us; the launch traced here: 44.4 us
  Pallas kernels  43.1 us (97%)
  local copies, waits for them, and re-layouts  1.3 us (3%)
    pallas_call x1, Pallas kernels, on_device(): pl.pallas_call(functools.partial(kernel, n, slots), out_shape=jax.ShapeDt...  43.1 us
    unnamed x1, local copies, waits for them, and re-layouts  1.3 us

profile of v1, /device:TPU:0, one launch (start us, length us, event | category | flops | bytes accessed | tf_op | source)
XLA Modules:
  0.0 44.4 jit_solution(9886730068399999050)
XLA Ops:
  0.0 43.1 %shard_map.64 = f32[12,128]{1,0:T(8,128)} custom-call(f32[12,128]{1,0:T(8,128)} %defect_ref.1, f32[12,128]{1,0:T(8,128)} %mass_ref.1, f32[12,128,128]{2,1,0:T(8,128)} %diag_hbm.1, f32[96,128,128]{2,1,0:T(8,128)} %coup_hbm.1, s32[1,96]{1,0:T(1,128)} %bitcast.2, s32[1,96]{1,0:T(1,128)} %bitcast.3), custom_call_target="tpu_custom_call" | custom-call | tf_op jit(solution)/shard_map/pallas_call | solution.py:392
  43.1 1.3 %copy.8 = f32[12,128]{1,0:T(8,128)} copy(f32[12,128]{1,0:T(8,128)} %shard_map.64) | data formatting | bytes 12288

commit v2 on v1

--- a/solution.py
+++ b/solution.py
@@ -10,7 +10,7 @@
 ITERS = 3
 F32 = jnp.float32
 MESH = pl.DeviceIdType.MESH
-STEP = 12
+STEP = 16
 
 
 def iota(shape, axis):
@@ -21,14 +21,17 @@
     return iota(shape, axis).astype(F32)
 
 
-def dot(a, b):
-    return lax.dot_general(
-        a,
-        b,
-        (((1,), (0,)), ((), ())),
-        precision=lax.Precision.HIGHEST,
-        preferred_element_type=F32,
-    )
+def dot(hot, value):
+    hot = hot.astype(jnp.bfloat16)
+    out = None
+    for _ in range(3):
+        piece = value.astype(jnp.bfloat16)
+        value = value - piece.astype(F32)
+        term = lax.dot_general(
+            hot, piece, (((1,), (0,)), ((), ())), preferred_element_type=F32
+        )
+        out = term if out is None else out + term
+    return out
 
 
 def total(value):
@@ -85,7 +88,7 @@
     tiles = rows_ref.shape[1]
     half = tiles // 2
     pad = wbuf.shape[0]
-    head = send0.shape[0]
+    head = send0.shape[1]
     parts = 4
     chunk = tiles // parts
 
@@ -100,13 +103,12 @@
 
     barrier = pltpu.get_barrier_semaphore()
 
-    def greet(k, carry):
-        pl.semaphore_signal(
-            barrier, inc=1, device_id=(lax.rem(me + k, n),), device_id_type=MESH
-        )
-        return carry
-
-    lax.fori_loop(1, n, greet, 0)
+    def peer(k):
+        there = me + k
+        return jnp.where(there >= n, there - n, there)
+
+    for k in range(1, n):
+        pl.semaphore_signal(barrier, inc=1, device_id=(peer(k),), device_id_type=MESH)
 
     rows = rows_ref[...]
     cols = cols_ref[...]
@@ -143,8 +145,9 @@
     own_s = to_s(own_l)
     far_s = to_s(far_l)
     loc_s = to_s(loc_l)
-    u_l = rel_l * 8.0 + slot_l
-    u_s = to_s(u_l)
+    lines = slots + 1
+    u_l = rel_l * lines + slot_l
+    u_s = to_s(rel_l * slots + slot_l)
     wide = (tiles, 128)
     lane_w = iota_f(wide, 1)
     push_int = jnp.where(pushes, 1, 0)
@@ -186,7 +189,8 @@
         axis=0,
         keepdims=True,
     ) - 1.0
-    slots8 = n * 8
+    lines_all = n * lines
+    slots_all = n * slots
 
     def hot(mask):
         return jnp.where(mask, 1.0, 0.0)
@@ -197,42 +201,40 @@
     mass16[0:rb, :] = mass_ref[...]
     vector = wbuf[...]
     send0[...] = jnp.zeros(send0.shape, F32)
-    send0[0:rb, :] = -defect_ref[...]
+    send0[0, 0:rb, :] = -defect_ref[...]
     own_part = as_row([total(vector * vector)])
-    send0[rb : rb + 1, :] = own_part
-    send0[rb + 1 : rb + 2, :] = asks
-    send0[rb + 2 : rb + 3, :] = goals
+    send0[0, rb : rb + 1, :] = own_part
+    send0[0, rb + 1 : rb + 2, :] = asks
+    send0[0, rb + 2 : rb + 3, :] = goals
     recv0[n - 1] = jnp.zeros(recv0.shape[1:], F32)
     for turn in range(ITERS):
-        recv_b[turn, n - 1] = jnp.zeros((8, 128), F32)
+        recv_b[turn, slots_all - slots : slots_all] = jnp.zeros((slots, 1, 128), F32)
     for turn in range(ITERS - 1):
-        recv_a[turn, n - 1] = jnp.zeros((8, 128), F32)
-    recv_f[n - 1] = jnp.zeros((8, 128), F32)
+        recv_a[turn, lines_all - lines : lines_all] = jnp.zeros((lines, 1, 128), F32)
+    recv_f[n - 1] = jnp.zeros((1, 128), F32)
 
     pl.semaphore_wait(barrier, n - 1)
 
-    def broadcast(source, target, index, spread):
-        def one(k, carry):
+    def broadcast(source, target, index, count, spread):
+        for k in range(1, n):
+            start = (n - 1 - k) * count
             pltpu.make_async_remote_copy(
-                src_ref=source.at[k - 1] if spread else source,
-                dst_ref=target.at[n - 1 - k],
+                src_ref=source.at[pl.ds((k - 1) * count, count)] if spread else source,
+                dst_ref=target.at[pl.ds(start, count)],
                 send_sem=sent.at[index],
                 recv_sem=got.at[index],
-                device_id=(lax.rem(me + k, n),),
+                device_id=(peer(k),),
                 device_id_type=MESH,
             ).start()
-            return carry
-
-        lax.fori_loop(1, n, one, 0)
-
-    def await_all(target, sem):
-        view = target.at[pl.ds(0, n - 1)]
+
+    def await_all(target, sem, count):
+        view = target.at[pl.ds(0, (n - 1) * count)]
         pltpu.make_async_copy(view, view, sem).wait()
 
-    broadcast(send0, recv0, 0, False)
-
-    spread_hot = hot(iota_f((slots8, 128), 0) == push_u)
-    fetch_hot = hot(iota_f((half, slots8), 1) == fetch_u)
+    broadcast(send0, recv0, 0, 1, False)
+
+    spread_hot = hot(iota_f((slots_all, 128), 0) == push_u)
+    fetch_hot = hot(iota_f((half, lines_all), 1) == fetch_u)
     first_hot = hot(iota_f((half, n * head), 1) == fetch_v)
     input_hot = hot(iota_f((half, pad), 1) == push_col)
     kept_hot = hot(iota_f((pad, 128), 0) == fetch_row)
@@ -258,47 +260,50 @@
 
     def begin(turn, vector):
         xbuf[0:half, :] = dot(input_hot, vector)
-        xbuf[half : half + pad, :] = vector
+        found = coupled(half, empty).T
+        send_b[turn, :, 0, :] = dot(spread_hot, found)
+        broadcast(send_b.at[turn], recv_b.at[turn], 1 + 2 * turn, slots, True)
+        wbuf[...] = vector
         acc = empty
         for index in range(rb):
-            acc = matvec(acc, diag[index], half + index)
-        acc = coupled(half, acc)
-        found = acc.T
-        send_b[turn] = dot(spread_hot, found).reshape(n, 8, 128)
-        broadcast(send_b.at[turn], recv_b.at[turn], 1 + 2 * turn, True)
-        return mass16[...] * vector + found[half : half + pad, :]
-
-    def finish(turn, image, inputs):
+            value = jnp.sum(diag[index] * wbuf[index : index + 1, :], axis=1, keepdims=True)
+            acc = jnp.where(lane_k == half + index, value, acc)
+        return mass16[...] * vector, acc
+
+    def finish(turn, started, inputs):
+        image, acc = started
         xbuf[0:half, :] = inputs
-        found = coupled(0, empty).T
-        image = image + dot(kept_hot, found)
-        await_all(recv_b.at[turn], got.at[1 + 2 * turn])
-        arrived = recv_b[turn].reshape(slots8, 128)
-        return image + dot(land_hot[...], arrived)
+        found = coupled(0, acc).T
+        image = image + dot(kept_hot, found) + found[half : half + pad, :]
+        await_all(recv_b.at[turn], got.at[1 + 2 * turn], slots)
+        return image + dot(land_hot[...], recv_b[turn, :, 0, :])
 
     for item in loads:
         item.wait()
     order_copy.wait()
 
-    image = begin(0, vector)
-    await_all(recv0, got.at[0])
-    lane_3 = iota((n, 8, 128), 2)
-    sub_3 = iota((n, 8, 128), 1)
-    peer_3 = iota((n, 8, 128), 0)
-    mine = (lane_3 == me * slots + sub_3) & (sub_3 < slots) & (peer_3 < n - 1)
-
-    def addressed(offset):
-        line = recv0[:, rb + offset : rb + offset + 1, :]
-        line = jnp.broadcast_to(line, (n, 8, 128))
-        found = jnp.sum(jnp.where(mine, line + 1.0, 0.0), axis=2, keepdims=True) - 1.0
-        return hot(found == lane_3.astype(F32)).reshape(slots8, 128)
-
-    land_hot[...] = addressed(2).T[0:pad, :]
-    ask_hot[...] = addressed(1)
+    started = begin(0, vector)
+    await_all(recv0, got.at[0], 1)
+
+    def addressed(offset, count):
+        size = n * count
+        line = recv0[:, rb + offset : rb + offset + 1, :].reshape(n, 128)
+        owner = jnp.floor((iota_f((size, n), 0) + 0.5) * (1.0 / count))
+        spread = dot(hot(owner == iota_f((size, n), 1)), line + 1.0)
+        row = iota_f((size, 128), 0)
+        owner = jnp.floor((row + 0.5) * (1.0 / count))
+        slot = row - owner * count
+        lane = iota_f((size, 128), 1)
+        mine = (lane == me_f * slots + slot) & (slot < slots) & (owner < n - 1)
+        found = jnp.sum(jnp.where(mine, spread, 0.0), axis=1, keepdims=True) - 1.0
+        return hot(found == lane)
+
+    land_hot[...] = addressed(2, slots).T[0:pad, :]
+    ask_hot[...] = addressed(1, lines)
     squares = jnp.sum(recv0[:, rb, :], axis=0, keepdims=True) + own_part
     beta = jnp.sqrt(pick(squares, 0))
     inputs = dot(first_hot, recv0[...].reshape(n * head, 128))
-    image = finish(0, image, inputs)
+    image = finish(0, started, inputs)
     basis = [vector / beta]
     images = [image / beta]
     heads = []
@@ -311,16 +316,17 @@
             + [total(vector * item) for item in images]
         )
         wide_vector = jnp.concatenate([vector, jnp.zeros((128 - pad, 128), F32)], axis=0)
-        blocks = dot(ask_hot[...], wide_vector).reshape(n, 8, 128)
-        sub = iota((n, 8, 128), 1)
-        blocks = jnp.where(sub == slots, own_part.reshape(1, 1, 128), blocks)
-        send_a[turn - 1] = blocks
-        broadcast(send_a.at[turn - 1], recv_a.at[turn - 1], 2 * turn, True)
-        image = begin(turn, vector)
-        await_all(recv_a.at[turn - 1], got.at[2 * turn])
-        sums = jnp.sum(recv_a[turn - 1][:, slots, :], axis=0, keepdims=True) + own_part
-        inputs = dot(fetch_hot, recv_a[turn - 1].reshape(slots8, 128))
-        image = finish(turn, image, inputs)
+        blocks = dot(ask_hot[...], wide_vector)
+        row = iota_f((lines_all, 128), 0)
+        slot = row - jnp.floor((row + 0.5) * (1.0 / lines)) * lines
+        send_a[turn - 1, :, 0, :] = jnp.where(slot == slots, own_part, blocks)
+        broadcast(send_a.at[turn - 1], recv_a.at[turn - 1], 2 * turn, lines, True)
+        started = begin(turn, vector)
+        await_all(recv_a.at[turn - 1], got.at[2 * turn], lines)
+        came = recv_a[turn - 1, :, 0, :]
+        sums = jnp.sum(jnp.where(slot == slots, came, 0.0), axis=0, keepdims=True)
+        sums = sums + own_part
+        image = finish(turn, started, dot(fetch_hot, came))
         dots = [pick(sums, index) for index in range(turn)]
         for index in range(turn):
             gram[index, turn - 1] = pick(sums, turn + index)
@@ -340,9 +346,9 @@
     own_part = as_row(
         [total(vector * basis[0])] + [total(vector * item) for item in images]
     )
-    send_f[...] = jnp.broadcast_to(own_part, (8, 128))
-    broadcast(send_f, recv_f, 2 * ITERS, False)
-    await_all(recv_f, got.at[2 * ITERS])
+    send_f[0] = own_part
+    broadcast(send_f, recv_f, 2 * ITERS, 1, False)
+    await_all(recv_f, got.at[2 * ITERS], 1)
     sums = jnp.sum(recv_f[:, 0, :], axis=0, keepdims=True) + own_part
     heads.append(pick(sums, 0))
     for index in range(ITERS):
@@ -372,12 +378,12 @@
         update = update + mixing[i] * basis[i]
     out_ref[...] = update[0:rb, :]
 
-    await_all(recv0, sent.at[0])
+    await_all(recv0, sent.at[0], 1)
     for turn in range(ITERS):
-        await_all(send_b.at[turn], sent.at[1 + 2 * turn])
+        await_all(send_b.at[turn], sent.at[1 + 2 * turn], slots)
     for turn in range(1, ITERS):
-        await_all(send_a.at[turn - 1], sent.at[2 * turn])
-    await_all(recv_f, sent.at[2 * ITERS])
+        await_all(send_a.at[turn - 1], sent.at[2 * turn], lines)
+    await_all(recv_f, sent.at[2 * ITERS], 1)
 
 
 def on_device(defect, mass, block_diag, coupling, tile_rows, tile_cols):
@@ -402,16 +408,16 @@
             pltpu.VMEM((pad, width), F32),
             pltpu.VMEM((pad, width), F32),
             pltpu.VMEM((tiles, width), F32),
-            pltpu.VMEM((n * 8, 128), F32),
-            pltpu.VMEM((pad, n * 8), F32),
-            pltpu.VMEM((head, width), F32),
+            pltpu.VMEM((n * (slots + 1), 128), F32),
+            pltpu.VMEM((pad, n * slots), F32),
+            pltpu.VMEM((1, head, width), F32),
             pltpu.VMEM((n, head, width), F32),
-            pltpu.VMEM((ITERS - 1, n, 8, width), F32),
-            pltpu.VMEM((ITERS - 1, n, 8, width), F32),
-            pltpu.VMEM((ITERS, n, 8, width), F32),
-            pltpu.VMEM((ITERS, n, 8, width), F32),
-            pltpu.VMEM((8, width), F32),
-            pltpu.VMEM((n, 8, width), F32),
+            pltpu.VMEM((ITERS - 1, n * (slots + 1), 1, width), F32),
+            pltpu.VMEM((ITERS - 1, n * (slots + 1), 1, width), F32),
+            pltpu.VMEM((ITERS, n * slots, 1, width), F32),
+            pltpu.VMEM((ITERS, n * slots, 1, width), F32),
+            pltpu.VMEM((1, 1, width), F32),
+            pltpu.VMEM((n, 1, width), F32),
             pltpu.SemaphoreType.DMA((5,)),
             pltpu.SemaphoreType.DMA,
             pltpu.SemaphoreType.DMA((2 * ITERS + 1,)),

time: 44.6 us -> 38.5 us (0.86)
  Pallas kernels: 43.1 us -> 36.9 us
    pallas_call x1, Pallas kernels: 43.1 us -> 36.9 us  [on_device(): pl.pallas_call(functools.partial(kernel, n, slots), out_shape=jax.ShapeDt...]
where the time goes in v2:
time: 38.5 us; the launch traced here: 38.2 us
  Pallas kernels  36.9 us (96%)
  local copies, waits for them, and re-layouts  1.3 us (3%)
    pallas_call x1, Pallas kernels, on_device(): pl.pallas_call(functools.partial(kernel, n, slots), out_shape=jax.ShapeDt...  36.9 us
    unnamed x1, local copies, waits for them, and re-layouts  1.3 us

profile of v2, /device:TPU:0, one launch (start us, length us, event | category | flops | bytes accessed | tf_op | source)
XLA Modules:
  0.0 38.2 jit_solution(14308432491422860469)
XLA Ops:
  0.0 36.9 %shard_map.64 = f32[12,128]{1,0:T(8,128)} custom-call(f32[12,128]{1,0:T(8,128)} %defect_ref.1, f32[12,128]{1,0:T(8,128)} %mass_ref.1, f32[12,128,128]{2,1,0:T(8,128)} %diag_hbm.1, f32[96,128,128]{2,1,0:T(8,128)} %coup_hbm.1, s32[1,96]{1,0:T(1,128)} %bitcast.2, s32[1,96]{1,0:T(1,128)} %bitcast.3), custom_call_target="tpu_custom_call" | custom-call | tf_op jit(solution)/shard_map/pallas_call | solution.py:398
  36.9 1.3 %copy.8 = f32[12,128]{1,0:T(8,128)} copy(f32[12,128]{1,0:T(8,128)} %shard_map.64) | data formatting | bytes 12288

commit v3 on v2

--- a/solution.py
+++ b/solution.py
@@ -10,7 +10,6 @@
 ITERS = 3
 F32 = jnp.float32
 MESH = pl.DeviceIdType.MESH
-STEP = 16
 
 
 def iota(shape, axis):
@@ -242,19 +241,15 @@
     lane_k = iota((width, 128), 1)
 
     def matvec(acc, tile, index):
-        row = xbuf[pl.ds(index, 1), :]
+        row = xbuf[index : index + 1, :]
         value = jnp.sum(tile * row, axis=1, keepdims=True)
         return jnp.where(lane_k == index, value, acc)
 
     def coupled(base, acc):
-        def body(step, acc):
-            for inner in range(STEP):
-                index = step * STEP + inner
-                tile = jnp.clip(order_s[0, base + index], 0, 2 * half - 1)
-                acc = matvec(acc, coup[tile], index)
-            return acc
-
-        return lax.fori_loop(0, half // STEP, body, acc)
+        for index in range(half):
+            tile = jnp.clip(order_s[0, base + index], 0, 2 * half - 1)
+            acc = matvec(acc, coup[tile], index)
+        return acc
 
     empty = jnp.zeros((width, 128), F32)
 

time: 38.5 us -> 37.9 us (0.984)
  Pallas kernels: 36.9 us -> 36.4 us
    pallas_call x1, Pallas kernels: 36.9 us -> 36.4 us  [on_device(): pl.pallas_call(functools.partial(kernel, n, slots), out_shape=jax.ShapeDt...]
where the time goes in v3:
time: 37.9 us; the launch traced here: 37.7 us
  Pallas kernels  36.4 us (96%)
  local copies, waits for them, and re-layouts  1.3 us (3%)
    pallas_call x1, Pallas kernels, on_device(): pl.pallas_call(functools.partial(kernel, n, slots), out_shape=jax.ShapeDt...  36.4 us
    unnamed x1, local copies, waits for them, and re-layouts  1.3 us

profile of v3, /device:TPU:0, one launch (start us, length us, event | category | flops | bytes accessed | tf_op | source)
XLA Modules:
  0.0 37.7 jit_solution(16521565179822553676)
XLA Ops:
  0.0 36.4 %shard_map.64 = f32[12,128]{1,0:T(8,128)} custom-call(f32[12,128]{1,0:T(8,128)} %defect_ref.1, f32[12,128]{1,0:T(8,128)} %mass_ref.1, f32[12,128,128]{2,1,0:T(8,128)} %diag_hbm.1, f32[96,128,128]{2,1,0:T(8,128)} %coup_hbm.1, s32[1,96]{1,0:T(1,128)} %bitcast.2, s32[1,96]{1,0:T(1,128)} %bitcast.3), custom_call_target="tpu_custom_call" | custom-call | tf_op jit(solution)/shard_map/pallas_call | solution.py:393
  36.4 1.3 %copy.8 = f32[12,128]{1,0:T(8,128)} copy(f32[12,128]{1,0:T(8,128)} %shard_map.64) | data formatting | bytes 12288
